TPU v7x, 32 devices: a whole 2x2x4 slice. The times are simulated.
32 devices in a mesh: seq: 32 (over z, y, x, core).
Axes of the slice: x: 2, y: 2, z: 4, core: 2. Of those that a mesh axis runs over, the one named last changes fastest.
Arguments:
- query: bfloat16 [32, 64, 128], replicated, may hold values from -8 to 8
- k_cache: bfloat16 [32, 6144, 1024], P(None, 'seq'), may hold values from -8 to 8
- v_cache: bfloat16 [32, 6144, 1024], P(None, 'seq'), may hold values from -16 to 16
- lengths: int32 [32], replicated, may hold values from 1 to 6144, as said below
Outputs:
- attended: float32 [2048, 128], P('seq')
Inputs may be any that keep to these rules, and one draw needn't show every extreme that they name: `lengths`: every length is between 1 and 6144; some sequence has length 6144 and some has length 1.
All inputs are finite; a program needn't handle non-finite values.
Results may differ from a plain program's by a relative error of at most 0.0028.
Values sent between devices are 32-bit elements.
A program may use at most 128 MiB of HBM per device.

v0:
```python
import jax
import jax.numpy as jnp
from jax import lax
from jax.sharding import PartitionSpec as P

masked_floor = -1e30


def local_partials(query, k_cache, v_cache, lengths):
    sequences, positions, columns = k_cache.shape
    heads = query.shape[1]
    head_size = query.shape[2]
    kv_heads = columns // head_size
    group_size = heads // kv_heads
    keys = k_cache.reshape(sequences, positions, kv_heads, head_size)
    values = v_cache.reshape(sequences, positions, kv_heads, head_size)
    grouped = query.reshape(sequences, kv_heads, group_size, head_size)
    scores = jnp.einsum(
        "bkgd,bpkd->bkgp", grouped, keys, preferred_element_type=jnp.float32
    ) * head_size ** (-0.5)
    offset = lax.axis_index("seq") * positions
    where_at = offset + lax.broadcasted_iota(jnp.int32, (sequences, 1, 1, positions), 3)
    valid = where_at < lengths.reshape(sequences, 1, 1, 1)
    scores = jnp.where(valid, scores, masked_floor)
    local_peak = jnp.max(scores, axis=3, keepdims=True)
    weights = jnp.where(valid, jnp.exp(scores - local_peak), 0.0)
    local_total = jnp.sum(weights, axis=3)
    rounded = weights.astype(jnp.bfloat16)
    weighted = jnp.einsum("bkgp,bpkd->bkgd", rounded, values, preferred_element_type=jnp.float32)
    row_count = sequences * heads
    return (
        local_peak.reshape(row_count),
        local_total.reshape(row_count),
        weighted.reshape(row_count, head_size),
    )


def body(query, k_cache, v_cache, lengths):
    local_peak, local_total, weighted = local_partials(query, k_cache, v_cache, lengths)
    row_count = weighted.shape[0]
    head_size = weighted.shape[1]
    devices = lax.axis_size("seq")
    share = row_count // devices
    got_peak, got_total, got_weighted = (
        lax.all_to_all(local_peak, "seq", split_axis=0, concat_axis=0, tiled=True),
        lax.all_to_all(local_total, "seq", split_axis=0, concat_axis=0, tiled=True),
        lax.all_to_all(weighted, "seq", split_axis=0, concat_axis=0, tiled=True),
    )
    got_peak = got_peak.reshape(devices, share)
    got_total = got_total.reshape(devices, share)
    got_weighted = got_weighted.reshape(devices, share, head_size)
    highest = jnp.max(got_peak, axis=0, keepdims=True)
    factor = jnp.exp(got_peak - highest)
    denom = jnp.sum(got_total * factor, axis=0)
    numer = jnp.sum(got_weighted * factor[:, :, None], axis=0)
    return numer / denom[:, None]


def solution(mesh):
    placed = (P(), P(None, "seq", None), P(None, "seq", None), P())
    return jax.shard_map(
        body, mesh=mesh, in_specs=placed, out_specs=P("seq", None), check_vma=False
    )
```

profile of v0, /device:TPU:0, one launch (start us, length us, event | category | flops | bytes accessed | tf_op | source)
XLA Modules:
  0.0 71.8 jit_solution(15295581553827677376)
XLA Ops:
  0.0 0.0 copy-start
  0.0 0.8 %broadcast_compare_fusion = pred[32,192]{1,0:T(8,128)(4,1)S(1)} fusion(s32[192]{0:T(256)S(1)} %iota_add_fusion, s32[32]{0:T(128)} %param.7), kind=kLoop, calls=%fused_computation.22 | loop fusion | flops 6144 | bytes 7040 | tf_op jit(solution)/shard_map/lt | solution.py:23
  0.8 0.3 copy-done
  1.1 9.7 %fusion.6 = (f32[32,8,8]{2,1,0:T(8,128)S(1)}, f32[32,8,8,192]{3,2,1,0:T(8,128)S(1)}) fusion(pred[32,192]{1,0:T(8,128)(4,1)S(1)} %broadcast_compare_fusion, bf16[32,64,128]{2,1,0:T(8,128)(2,1)S(1)} %copy-done, bf16[32,192,1024]{2,1,0:T(8,128)(2,1)} %param.5), kind=kOutput, calls=%fused_computation.8 | convolution fusion | flops 101840896 | bytes 14694400 | tf_op jit(solution)/shard_map/bkgd,bpkd->bkgp/dot_general | solution.py:18
  10.7 1.1 %fusion.7 = f32[32,8,8]{2,1,0:T(8,128)S(1)} fusion(f32[32,8,8,192]{3,2,1,0:T(8,128)S(1)} %get-tuple-element.6, f32[32,8,8]{2,1,0:T(8,128)S(1)} %get-tuple-element.5, pred[32,192]{1,0:T(8,128)(4,1)S(1)} %broadcast_compare_fusion), kind=kLoop, calls=%fused_computation.9 | loop fusion | flops 1964032 | bytes 1595392 | tf_op jit(solution)/shard_map/reduce_sum | solution.py:27
  11.8 0.1 copy.15
  11.9 0.7 copy.16
  12.6 7.3 %all-to-all-start.2 = ((f32[32,64,1]{1,2,0:T(1,128)}), f32[32,64,1]{1,2,0:T(1,128)S(1)}, u32[]{:S(2)}, u32[]{:S(2)}) async-start(f32[32,64,1]{1,2,0:T(1,128)} %copy.16), calls=%async_computation.2 | async-start | bytes 32768 | tf_op jit(solution)/shard_map/all_to_all | solution.py:46
  19.9 0.1 copy.13
  20.0 0.7 copy.14
  20.7 6.4 %all-to-all-done.2 = f32[32,64,1]{1,2,0:T(1,128)S(1)} async-done(((f32[32,64,1]{1,2,0:T(1,128)}), f32[32,64,1]{1,2,0:T(1,128)S(1)}, u32[]{:S(2)}, u32[]{:S(2)}) %all-to-all-start.2) | async-done | bytes 8224 | tf_op jit(solution)/shard_map/all_to_all | solution.py:46
  27.1 2.5 %all-to-all-start.1 = ((f32[32,64,1]{1,2,0:T(1,128)}), f32[32,64,1]{1,2,0:T(1,128)S(1)}, u32[]{:S(2)}, u32[]{:S(2)}) async-start(f32[32,64,1]{1,2,0:T(1,128)} %copy.14), calls=%async_computation.1 | async-start | bytes 32768 | tf_op jit(solution)/shard_map/all_to_all | solution.py:45
  29.6 9.1 %fusion.9 = f32[32,64,128]{2,1,0:T(8,128)} fusion(f32[32,8,8,192]{3,2,1,0:T(8,128)S(1)} %get-tuple-element.6, f32[32,8,8]{2,1,0:T(8,128)S(1)} %get-tuple-element.5, pred[32,192]{1,0:T(8,128)(4,1)S(1)} %broadcast_compare_fusion, bf16[32,192,1024]{2,1,0:T(8,128)(2,1)} %param.6), kind=kOutput, calls=%fused_computation.11 | convolution fusion | flops 102629376 | bytes 15218688 | tf_op jit(solution)/shard_map/bkgp,bpkd->bkgd/dot_general | solution.py:29
  38.7 0.0 all-to-all-done.1
  38.7 5.8 %all-to-all-start = ((f32[32,64,128]{2,1,0:T(8,128)}), f32[32,64,128]{2,1,0:T(8,128)S(1)}, u32[]{:S(2)}, u32[]{:S(2)}) async-start(f32[32,64,128]{2,1,0:T(8,128)} %fusion.9), calls=%async_computation | async-start | bytes 2097152 | tf_op jit(solution)/shard_map/all_to_all | solution.py:47
  44.5 0.1 reduce_max.19
  44.7 26.1 %all-to-all-done = f32[32,64,128]{2,1,0:T(8,128)S(1)} async-done(((f32[32,64,128]{2,1,0:T(8,128)}), f32[32,64,128]{2,1,0:T(8,128)S(1)}, u32[]{:S(2)}, u32[]{:S(2)}) %all-to-all-start) | async-done | bytes 1048608 | tf_op jit(solution)/shard_map/all_to_all | solution.py:47
  70.7 0.3 multiply_reduce_fusion
  71.1 0.7 broadcast_divide_fusion
  (3 shorter events, 0.1 us)
Async XLA Ops:
  0.0 1.1 %copy-start = (bf16[32,64,128]{2,1,0:T(8,128)(2,1)S(1)}, bf16[32,64,128]{2,1,0:T(8,128)(2,1)}, u32[]{:S(2)}) copy-start(bf16[32,64,128]{2,1,0:T(8,128)(2,1)} %param.4) | copy-start | bytes 1572868
  12.6 14.5 %all-to-all-start.2 = ((f32[32,64,1]{1,2,0:T(1,128)}), f32[32,64,1]{1,2,0:T(1,128)S(1)}, u32[]{:S(2)}, u32[]{:S(2)}) async-start(f32[32,64,1]{1,2,0:T(1,128)} %copy.16), calls=%async_computation.2 | async-start | bytes 32768 | tf_op jit(solution)/shard_map/all_to_all | solution.py:46
  27.1 11.6 %all-to-all-start.1 = ((f32[32,64,1]{1,2,0:T(1,128)}), f32[32,64,1]{1,2,0:T(1,128)S(1)}, u32[]{:S(2)}, u32[]{:S(2)}) async-start(f32[32,64,1]{1,2,0:T(1,128)} %copy.14), calls=%async_computation.1 | async-start | bytes 32768 | tf_op jit(solution)/shard_map/all_to_all | solution.py:45
  38.7 32.0 %all-to-all-start = ((f32[32,64,128]{2,1,0:T(8,128)}), f32[32,64,128]{2,1,0:T(8,128)S(1)}, u32[]{:S(2)}, u32[]{:S(2)}) async-start(f32[32,64,128]{2,1,0:T(8,128)} %fusion.9), calls=%async_computation | async-start | bytes 2097152 | tf_op jit(solution)/shard_map/all_to_all | solution.py:47
where the time goes:
time: 72.1 us; the launch traced here: 71.8 us
  waiting for transfers between devices  32.5 us (45%)
  matrix products  18.7 us (26%)
  starting transfers between devices  15.7 us (22%)
  other arithmetic  3.01 us (4%)
  local copies, waits for them, and re-layouts  1.84 us (3%)
    all_to_all x1, waiting for transfers between devices, body(): lax.all_to_all(weighted, 'seq', split_axis=0, concat_axis=0, tiled=True)  26.1 us
    dot_general x1, matrix products, local_partials(): jnp.einsum('bkgd,bpkd->bkgp', grouped, keys, preferred_element_type=jnp.f...  9.66 us
    dot_general x1, matrix products, local_partials(): jnp.einsum('bkgp,bpkd->bkgd', rounded, values, preferred_element_type=jnp...  9.06 us
    all_to_all x1, starting transfers between devices, body(): lax.all_to_all(local_total, 'seq', split_axis=0, concat_axis=0, tiled=True)  7.33 us
    all_to_all x1, waiting for transfers between devices, body(): lax.all_to_all(local_total, 'seq', split_axis=0, concat_axis=0, tiled=True)  6.38 us
    all_to_all x1, starting transfers between devices, body(): lax.all_to_all(weighted, 'seq', split_axis=0, concat_axis=0, tiled=True)  5.83 us
    all_to_all x1, starting transfers between devices, body(): lax.all_to_all(local_peak, 'seq', split_axis=0, concat_axis=0, tiled=True)  2.54 us
  transfers between devices with their start and end apart: 3, of which 2 were waited for; matrix products, arithmetic and copies ran while one was open for 14% of the time, Pallas kernels for 0%

commit v1 on v0

v1 whole, which is shorter than its diff:
```python
import functools

import jax
import jax.numpy as jnp
from jax import lax
from jax.experimental import pallas as pl
from jax.experimental.pallas import tpu as pltpu
from jax.sharding import PartitionSpec as P

masked_floor = -1e30
LEAD = 3
BLOCK = 2
DELAY = 1


def low_bit(j):
    return j & -j


def merge_order(count):
    order = []
    step = 2
    while step < count:
        order += [d for d in range(count - 1, 0, -1) if low_bit(d) == step]
        step *= 2
    return order + [0]


def plan(count):
    evens = merge_order(count)
    odds = [d + 1 for d in evens]
    computes = odds[:LEAD]
    for i, d in enumerate(evens):
        if i + LEAD < len(odds):
            computes.append(odds[i + LEAD])
        computes.append(d)
    blocks = [computes[i : i + BLOCK] for i in range(0, len(computes), BLOCK)]
    merges = [[] for _ in range(len(blocks) + DELAY)]
    for i, block in enumerate(blocks):
        merges[i + DELAY] += [d for d in block if d % 2 == 0 and d != 0]
    return blocks, merges


def kernel(
    devices, kv_heads, final,
    lengths_ref, q_hbm, k_hbm, v_hbm, out_ref,
    qbuf, kbuf, vbuf, acc, got,
    q_sem, k_sem, v_sem, send_sem, recv_sem,
):
    sequences, heads, head_size = qbuf.shape
    positions = kbuf.shape[1]
    group = heads // kv_heads
    me = lax.axis_index("seq")
    spread = devices // sequences
    mine = me // spread
    rest = me % spread
    bits = sequences.bit_length() - 1

    def target(d):
        total = 0
        for k in range(bits):
            bit = (mine // (1 << k)) % 2
            if d >> k & 1:
                bit = 1 - bit
            total = total + bit * (1 << k)
        return total

    barrier = pltpu.get_barrier_semaphore()
    partners = [target(1 << k) * spread + rest for k in range(bits)]
    blocks, merges = plan(sequences)

    copies = {}
    q_copy = pltpu.make_async_copy(q_hbm, qbuf, q_sem)
    q_copy.start()
    for block in blocks:
        for d in block:
            t = target(d)
            copies[d] = (
                pltpu.make_async_copy(k_hbm.at[t], kbuf.at[d], k_sem.at[d]),
                pltpu.make_async_copy(v_hbm.at[t], vbuf.at[d], v_sem.at[d]),
            )
            copies[d][0].start()
            copies[d][1].start()
    for partner in partners:
        pl.semaphore_signal(
            barrier, inc=1, device_id=(partner,), device_id_type=pl.DeviceIdType.MESH
        )
    q_copy.wait()

    lane = lax.broadcasted_iota(jnp.int32, (group, 128), 1)
    row = lax.broadcasted_iota(jnp.int32, (2 * group, head_size), 0)
    upper = jnp.where(row < group, 1.0, 0.0).astype(jnp.bfloat16)
    lower = jnp.where(row < group, 0.0, 1.0).astype(jnp.bfloat16)
    where_at = me * positions + lax.broadcasted_iota(jnp.int32, (2 * group, positions), 1)
    scale = head_size ** (-0.5)

    def compute(d):
        t = target(d)
        length = lengths_ref[t]
        valid = where_at < length
        stat = jnp.zeros((group, 128), jnp.float32)
        scores = []
        for j in range(kv_heads // 2):
            q = qbuf[t, pl.ds(2 * group * j, 2 * group), :]
            paired = jnp.concatenate([q * upper, q * lower], axis=1)
            scores.append(
                lax.dot_general(
                    paired,
                    kbuf[d, :, pl.ds(2 * head_size * j, 2 * head_size)],
                    (((1,), (1,)), ((), ())),
                    preferred_element_type=jnp.float32,
                )
            )
        for j in range(kv_heads // 2):
            score = jnp.where(valid, scores[j] * scale, masked_floor)
            peak = jnp.max(score, axis=1, keepdims=True)
            weight = jnp.where(valid, jnp.exp(score - peak), 0.0)
            total = jnp.sum(weight, axis=1, keepdims=True)
            result = jnp.dot(
                weight.astype(jnp.bfloat16),
                vbuf[d, :, pl.ds(2 * head_size * j, 2 * head_size)],
                preferred_element_type=jnp.float32,
            )
            for u in range(2):
                k = 2 * j + u
                rows = slice(group * u, group * (u + 1))
                acc[d, pl.ds(group * k, group), :] = result[rows, head_size * u : head_size * (u + 1)]
                stat = jnp.where(lane == k, peak[rows], stat)
                stat = jnp.where(lane == kv_heads + k, total[rows], stat)
        acc[d, pl.ds(heads, group), :] = stat

    def sending(d):
        k = low_bit(d).bit_length() - 1
        return pltpu.make_async_remote_copy(
            src_ref=acc.at[d],
            dst_ref=got.at[d],
            send_sem=send_sem.at[d],
            recv_sem=recv_sem.at[d],
            device_id=(partners[k],),
            device_id_type=pl.DeviceIdType.MESH,
        )

    def sources(d):
        limit = low_bit(d) if d else sequences
        found, step = [], 1
        while step < limit:
            found.append(d + step)
            step *= 2
        return found

    def merged(d, others):
        stats = [acc[d, pl.ds(heads, group), :]] + [got[j, pl.ds(heads, group), :] for j in others]
        top = functools.reduce(jnp.maximum, stats)
        factors = [jnp.exp(s - top) for s in stats]
        total = sum(s * pltpu.roll(f, kv_heads, 1) for s, f in zip(stats, factors))
        stat = jnp.where(lane < kv_heads, top, total)
        parts = []
        for k in range(kv_heads):
            rows = pl.ds(group * k, group)
            values = [acc[d, rows, :]] + [got[j, rows, :] for j in others]
            parts.append(sum(v * f[:, k : k + 1] for v, f in zip(values, factors)))
        return parts, stat

    def merge(d, others):
        parts, stat = merged(d, others)
        for k in range(kv_heads):
            acc[d, pl.ds(group * k, group), :] = parts[k]
        acc[d, pl.ds(heads, group), :] = stat

    first = True
    for i in range(len(merges)):
        block = blocks[i] if i < len(blocks) else []
        for d in block:
            copies[d][0].wait()
            copies[d][1].wait()
        for d in merges[i]:
            for j in sources(d):
                sending(j).wait_recv()
        for d in block:
            compute(d)
        for d in merges[i]:
            merge(d, sources(d))
        if first:
            pl.semaphore_wait(barrier, bits)
            first = False
        for d in merges[i] + [d for d in block if d % 2]:
            sending(d).start()

    early, late = sources(0)[:-2], sources(0)[-2:]
    for j in early:
        sending(j).wait_recv()
    merge(0, early)
    for j in late:
        sending(j).wait_recv()
    parts, stat = merged(0, late)
    for k in range(kv_heads):
        if final:
            parts[k] = parts[k] / stat[:, kv_heads + k : kv_heads + k + 1]
        out_ref[pl.ds(group * k, group), :] = parts[k]
    if not final:
        out_ref[pl.ds(heads, group), :] = stat
    for d in range(1, sequences):
        sending(d).wait_send()


def body(devices, query, k_cache, v_cache, lengths):
    sequences, heads, head_size = query.shape
    positions, columns = k_cache.shape[1:]
    kv_heads = columns // head_size
    group = heads // kv_heads
    spread = devices // sequences
    final = spread == 1
    rows = heads if final else heads + group
    anywhere = pl.BlockSpec(memory_space=pl.ANY)
    out = pl.pallas_call(
        functools.partial(kernel, devices, kv_heads, final),
        out_shape=jax.ShapeDtypeStruct((rows, head_size), jnp.float32),
        in_specs=[pl.BlockSpec(memory_space=pltpu.SMEM), anywhere, anywhere, anywhere],
        out_specs=pl.BlockSpec(memory_space=pltpu.VMEM),
        scratch_shapes=[
            pltpu.VMEM(query.shape, query.dtype),
            pltpu.VMEM(k_cache.shape, k_cache.dtype),
            pltpu.VMEM(v_cache.shape, v_cache.dtype),
            pltpu.VMEM((sequences, heads + group, head_size), jnp.float32),
            pltpu.VMEM((sequences, heads + group, head_size), jnp.float32),
            pltpu.SemaphoreType.DMA,
            pltpu.SemaphoreType.DMA((sequences,)),
            pltpu.SemaphoreType.DMA((sequences,)),
            pltpu.SemaphoreType.DMA((sequences,)),
            pltpu.SemaphoreType.DMA((sequences,)),
        ],
        compiler_params=pltpu.CompilerParams(
            collective_id=0, has_side_effects=True, vmem_limit_bytes=56 * 1024 * 1024
        ),
    )(lengths, query, k_cache, v_cache)
    if final:
        return out
    share = heads // spread
    rest = lax.axis_index("seq") % spread
    weighted = out[:heads]
    peak = out[heads:, :kv_heads].T.reshape(heads, 1)
    total = out[heads:, kv_heads : 2 * kv_heads].T.reshape(heads, 1)
    packed = jnp.concatenate([weighted, peak, total], axis=1)
    pieces = []
    for shift in range(spread):
        piece = lax.dynamic_slice_in_dim(packed, (rest + shift) % spread * share, share, 0)
        if shift:
            moves = [(i, i // spread * spread + (i + shift) % spread) for i in range(devices)]
            piece = lax.ppermute(piece, "seq", moves)
        pieces.append(piece)
    pieces = jnp.stack(pieces)
    factor = jnp.exp(pieces[:, :, head_size] - jnp.max(pieces[:, :, head_size], axis=0))
    denom = jnp.sum(pieces[:, :, head_size + 1] * factor, axis=0)
    numer = jnp.sum(pieces[:, :, :head_size] * factor[:, :, None], axis=0)
    return numer / denom[:, None]


def solution(mesh):
    placed = (P(), P(None, "seq", None), P(None, "seq", None), P())
    return jax.shard_map(
        functools.partial(body, mesh.shape["seq"]),
        mesh=mesh, in_specs=placed, out_specs=P("seq", None), check_vma=False,
    )
```

time: 72.1 us -> 37.8 us (0.52)
  Pallas kernels: 0 us -> 36.3 us
  waiting for transfers between devices: 32.5 us -> 0 us
  matrix products: 18.7 us -> 0 us
  starting transfers between devices: 15.7 us -> 0 us
  other arithmetic: 3.01 us -> 0 us
    pallas_call x0 -> x1, Pallas kernels: none -> 36.3 us  [body(): pl.pallas_call(functools.partial(kernel, devices, kv_heads, final), out_s...]
    all_to_all x3 -> x0, waiting for transfers between devices: 32.5 us -> none  [the longest x1 26.1 us: body(): lax.all_to_all(weighted, 'seq', split_axis=0, concat_axis=0, tiled=True)]
    dot_general x2 -> x0, matrix products: 18.7 us -> none  [the longest x1 9.66 us: local_partials(): jnp.einsum('bkgd,bpkd->bkgp', grouped, keys, preferred_element_type=jnp.f...]
    all_to_all x3 -> x0, starting transfers between devices: 15.7 us -> none  [the longest x1 7.33 us: body(): lax.all_to_all(local_total, 'seq', split_axis=0, concat_axis=0, tiled=True)]
    reduce_sum x3 -> x0, other arithmetic: 1.44 us -> none  [the longest x1 1.07 us: local_partials(): local_total = jnp.sum(weights, axis=3)]
    all_to_all x2 -> x0, local copies, waits for them, and re-layouts: 1.38 us -> none  [the longest x1 0.69 us: body(): lax.all_to_all(local_peak, 'seq', split_axis=0, concat_axis=0, tiled=True)]
    unnamed x2 -> x1, local copies, waits for them, and re-layouts: 0.27 us -> 1.38 us
    lt x1 -> x0, other arithmetic: 0.79 us -> none  [local_partials(): valid = where_at < lengths.reshape(sequences, 1, 1, 1)]
  transfers between devices with their start and end apart: 3 -> 0, of which waited for: 2 -> 0; matrix products, arithmetic and copies ran while one was open for 14% -> 0% of each run, Pallas kernels for 0% -> 0%
where the time goes in v1:
time: 37.8 us; the launch traced here: 37.6 us
  Pallas kernels  36.3 us (96%)
  local copies, waits for them, and re-layouts  1.38 us (4%)
    pallas_call x1, Pallas kernels, body(): pl.pallas_call(functools.partial(kernel, devices, kv_heads, final), out_s...  36.3 us
    unnamed x1, local copies, waits for them, and re-layouts  1.38 us

profile of v1, /device:TPU:0, one launch (start us, length us, event | category | flops | bytes accessed | tf_op | source)
XLA Modules:
  0.0 37.6 jit_solution(15814382596389613139)
XLA Ops:
  0.0 36.3 %shard_map.46 = f32[64,128]{1,0:T(8,128)} custom-call(s32[32]{0:T(128)} %lengths_ref.1, bf16[32,64,128]{2,1,0:T(8,128)(2,1)} %q_hbm.1, bf16[32,192,1024]{2,1,0:T(8,128)(2,1)} %k_hbm.1, bf16[32,192,1024]{2,1,0:T(8,128)(2,1)} %v_hbm.1), custom_call_target="tpu_custom_call" | custom-call | tf_op jit(solution)/shard_map/pallas_call | solution.py:215
  36.3 1.4 %copy.6 = f32[64,128]{1,0:T(8,128)} copy(f32[64,128]{1,0:T(8,128)} %shard_map.46) | data formatting | bytes 65536

commit v2 on v1

--- a/solution.py
+++ b/solution.py
@@ -9,20 +9,55 @@
 
 masked_floor = -1e30
 LEAD = 3
-BLOCK = 2
-DELAY = 1
-
-
-def low_bit(j):
-    return j & -j
+BLOCK = 4
+DELAY = 0
+HOP = 4
+LATE = True
+EARLY = 4
+AHEAD = 8
+
+
+def stages(count):
+    bits = count.bit_length() - 1
+    found, low = [(0, 1)], 1
+    while low < bits:
+        size = min(2, bits - low)
+        found.append((low, size))
+        low += size
+    return found
+
+
+def digits(d, count):
+    return [(low, d >> low & ((1 << size) - 1)) for low, size in stages(count)]
+
+
+def hop(d, count):
+    low, value = next(pair for pair in digits(d, count) if pair[1])
+    return value << low
+
+
+def sources(d, count):
+    found = []
+    for low, size in stages(count):
+        if d >> low & ((1 << size) - 1):
+            break
+        found += [d + (value << low) for value in range(1, 1 << size)]
+    return found
 
 
 def merge_order(count):
-    order = []
-    step = 2
-    while step < count:
-        order += [d for d in range(count - 1, 0, -1) if low_bit(d) == step]
-        step *= 2
+    waiting = list(range(count - 2, 0, -2))
+    ready, order = {}, []
+
+    def when(d):
+        return max([ready.get(j, 99) for j in sources(d, count) if j % 2 == 0] or [-99])
+
+    while waiting:
+        free = [d for d in waiting if when(d) + HOP <= len(order)] or [min(waiting, key=when)]
+        pick = max(free, key=lambda d: (sum(value > 0 for _, value in digits(d, count)), d))
+        ready[pick] = len(order)
+        order.append(pick)
+        waiting.remove(pick)
     return order + [0]
 
 
@@ -56,17 +91,14 @@
     rest = me % spread
     bits = sequences.bit_length() - 1
 
+    own = [(mine // (1 << k)) % 2 for k in range(bits)]
+
     def target(d):
-        total = 0
-        for k in range(bits):
-            bit = (mine // (1 << k)) % 2
-            if d >> k & 1:
-                bit = 1 - bit
-            total = total + bit * (1 << k)
-        return total
+        return sum((own[k] + (d >> k & 1)) % 2 * (1 << k) for k in range(bits))
 
     barrier = pltpu.get_barrier_semaphore()
-    partners = [target(1 << k) * spread + rest for k in range(bits)]
+    steps = [value << low for low, size in stages(sequences) for value in range(1, 1 << size)]
+    partners = [target(step) * spread + rest for step in steps]
     blocks, merges = plan(sequences)
 
     copies = {}
@@ -79,8 +111,14 @@
                 pltpu.make_async_copy(k_hbm.at[t], kbuf.at[d], k_sem.at[d]),
                 pltpu.make_async_copy(v_hbm.at[t], vbuf.at[d], v_sem.at[d]),
             )
+    order = [d for block in blocks for d in block]
+
+    def fetch(places):
+        for d in order[places]:
             copies[d][0].start()
             copies[d][1].start()
+
+    fetch(slice(0, AHEAD))
     for partner in partners:
         pl.semaphore_signal(
             barrier, inc=1, device_id=(partner,), device_id_type=pl.DeviceIdType.MESH
@@ -130,23 +168,14 @@
         acc[d, pl.ds(heads, group), :] = stat
 
     def sending(d):
-        k = low_bit(d).bit_length() - 1
         return pltpu.make_async_remote_copy(
             src_ref=acc.at[d],
             dst_ref=got.at[d],
             send_sem=send_sem.at[d],
             recv_sem=recv_sem.at[d],
-            device_id=(partners[k],),
+            device_id=(target(hop(d, sequences)) * spread + rest,),
             device_id_type=pl.DeviceIdType.MESH,
         )
-
-    def sources(d):
-        limit = low_bit(d) if d else sequences
-        found, step = [], 1
-        while step < limit:
-            found.append(d + step)
-            step *= 2
-        return found
 
     def merged(d, others):
         stats = [acc[d, pl.ds(heads, group), :]] + [got[j, pl.ds(heads, group), :] for j in others]
@@ -173,20 +202,32 @@
         for d in block:
             copies[d][0].wait()
             copies[d][1].wait()
+        fetch(slice(i * BLOCK + AHEAD, (i + 1) * BLOCK + AHEAD))
+        if LATE:
+            for d in block:
+                compute(d)
+            if first:
+                pl.semaphore_wait(barrier, len(partners))
+                first = False
+            for d in block:
+                if d % 2:
+                    sending(d).start()
         for d in merges[i]:
-            for j in sources(d):
+            for j in sources(d, sequences):
                 sending(j).wait_recv()
-        for d in block:
-            compute(d)
+        if not LATE:
+            for d in block:
+                compute(d)
         for d in merges[i]:
-            merge(d, sources(d))
+            merge(d, sources(d, sequences))
         if first:
-            pl.semaphore_wait(barrier, bits)
+            pl.semaphore_wait(barrier, len(partners))
             first = False
-        for d in merges[i] + [d for d in block if d % 2]:
+        for d in merges[i] + [d for d in block if d % 2 and not LATE]:
             sending(d).start()
 
-    early, late = sources(0)[:-2], sources(0)[-2:]
+    others = sources(0, sequences)
+    early, late = others[:EARLY], others[EARLY:]
     for j in early:
         sending(j).wait_recv()
     merge(0, early)

time: 37.8 us -> 24.5 us (0.65)
  Pallas kernels: 36.3 us -> 23 us
    pallas_call x1, Pallas kernels: 36.3 us -> 23 us  [body(): pl.pallas_call(functools.partial(kernel, devices, kv_heads, final), out_s...]
where the time goes in v2:
time: 24.5 us; the launch traced here: 24.4 us
  Pallas kernels  23 us (94%)
  local copies, waits for them, and re-layouts  1.38 us (6%)
    pallas_call x1, Pallas kernels, body(): pl.pallas_call(functools.partial(kernel, devices, kv_heads, final), out_s...  23 us
    unnamed x1, local copies, waits for them, and re-layouts  1.38 us

profile of v2, /device:TPU:0, one launch (start us, length us, event | category | flops | bytes accessed | tf_op | source)
XLA Modules:
  0.0 24.4 jit_solution(6549195262822362022)
XLA Ops:
  0.0 23.0 %shard_map.46 = f32[64,128]{1,0:T(8,128)} custom-call(s32[32]{0:T(128)} %lengths_ref.1, bf16[32,64,128]{2,1,0:T(8,128)(2,1)} %q_hbm.1, bf16[32,192,1024]{2,1,0:T(8,128)(2,1)} %k_hbm.1, bf16[32,192,1024]{2,1,0:T(8,128)(2,1)} %v_hbm.1), custom_call_target="tpu_custom_call" | custom-call | tf_op jit(solution)/shard_map/pallas_call | solution.py:256
  23.0 1.4 %copy.6 = f32[64,128]{1,0:T(8,128)} copy(f32[64,128]{1,0:T(8,128)} %shard_map.46) | data formatting | bytes 65536
